TPU v7x, 32 devices: a whole 2x2x4 slice. The times are simulated.
32 devices in a mesh: row: 16 (over z, y, x), col: 2 (over core).
Axes of the slice: x: 2, y: 2, z: 4, core: 2. Of those that a mesh axis runs over, the one named last changes fastest.
Arguments:
- block_ids: int32 [64, 8], replicated, may hold values from 0 to 383, as said below
- iface_counts: int32 [64], replicated, may hold values from 6 to 8
- inv_factor: bfloat16 [30208, 472], P(('row', 'col')), as said below
- coupling: bfloat16 [30208, 1024], P(('row', 'col')), may hold values from -0.375 to 0.375
- boundary_block: bfloat16 [24, 2048, 8, 256], P(None, 'row', None, 'col'), may hold values from -6 to 6
Outputs:
- schur: float32 [24, 2048, 8, 256], P(None, 'row', None, 'col')
Inputs may be any that keep to these rules, and one draw needn't show every extreme that they name: For j < 2, block_ids[s, j] is below 16, equals (s // 2 + j) modulo 2, and is the same for the 2 substructures that share s // 2. Apart from these shared first 2 ids, the ids of the 2 substructures that share s // 2 are distinct modulo 16. `inv_factor`: each substructure's block is lower triangular with a diagonal from 0.5 to 1.5.
All inputs are finite; a program needn't handle non-finite values.
Results may differ from a plain program's by a relative error of at most 0.00044.
Values sent between devices are 32-bit elements; how exact they have to be, the bound alone decides.
A program may use at most 64 MiB of HBM per device.

v0:
```python
import functools

import jax
import jax.numpy as jnp
from jax import lax
from jax.experimental import pallas as pl
from jax.experimental.pallas import tpu as pltpu
from jax.sharding import PartitionSpec as P

CS = 2
MESH = pl.DeviceIdType.MESH


def exchange_kernel(
    rows, cols, members, slots, width, nq, cq,
    pieces,
    ids_ref, counts_ref, factor_ref, couple_ref, boundary_ref,
    out_ref,
    w_ref, k_ref, y_ref, p_ref, send_ref, recv_ref, given_ref, place_ref,
    load_sem, send_sem, recv_sem, given_sem,
):
    row_at = lax.axis_index("row")
    col_at = lax.axis_index("col")
    half = rows // 2
    side = row_at // half

    loads = []
    for m in range(members):
        loads.append(
            (
                pltpu.make_async_copy(factor_ref.at[m], w_ref.at[m], load_sem.at[2 * m]),
                pltpu.make_async_copy(couple_ref.at[m], k_ref.at[m], load_sem.at[2 * m + 1]),
            )
        )
        for load in loads[-1]:
            load.start()

    barrier = pltpu.get_barrier_semaphore()
    for r in range(1, rows):
        other = lax.rem(row_at + r, rows)
        pl.semaphore_signal(barrier, inc=1, device_id=(other, col_at), device_id_type=MESH)
    for r in range(rows):
        for j in range(1, CS):
            pl.semaphore_signal(
                barrier, inc=1, device_id=(r, lax.rem(col_at + j, cols)), device_id_type=MESH
            )
            if cols > 2:
                pl.semaphore_signal(
                    barrier, inc=1, device_id=(r, lax.rem(col_at + cols - j, cols)),
                    device_id_type=MESH,
                )

    given = pltpu.make_async_copy(boundary_ref, given_ref, given_sem)
    given.start()

    own = (row_at * cols + col_at) * members
    for m in range(members):
        for load in loads[m]:
            load.wait()
        for n in range(0, slots * 128, 256):
            y_ref[m, :, n : n + 256] = jnp.dot(
                w_ref[m], k_ref[m, :, n : n + 256], preferred_element_type=jnp.float32
            ).astype(jnp.bfloat16)
        for n in range(0, slots, 2):
            part = lax.dot_general(
                y_ref[m, :, n * 128 : n * 128 + 256],
                y_ref[m, :, 0 : CS * 128],
                (((0,), (0,)), ((), ())),
                preferred_element_type=jnp.float32,
            )
            for d in range(2):
                for j in range(CS):
                    p_ref[m * slots + n + d, j] = part[
                        d * 128 : (d + 1) * 128, j * 128 : (j + 1) * 128
                    ]

    targets = []
    for i in range(half):
        targets.append((1 - side) * half + lax.rem(row_at + i, half))
        targets.append(side * half + lax.rem(row_at + i + 1, half))

    partners = (rows - 1) + (CS - 1) * rows * (2 if cols > 2 else 1)
    def route(i, target, j, piece):
        start, height = pieces[piece]
        src = send_ref.at[pl.ds((j * rows + i) * 128 + start, height)]
        dst = recv_ref.at[pl.ds((j * rows + row_at) * 128 + start, height)]
        if j == 0 and i == rows - 1:
            return pltpu.make_async_copy(src, dst, recv_sem.at[piece])
        return pltpu.make_async_remote_copy(
            src_ref=src,
            dst_ref=dst,
            send_sem=send_sem,
            recv_sem=recv_sem.at[piece],
            device_id=(target, lax.rem(col_at + j, cols)),
            device_id_type=MESH,
        )

    for i, target in enumerate(targets):
        picks = []
        for m in range(members):
            k, weight = jnp.int32(0), jnp.float32(0.0)
            count = counts_ref[own + m]
            for kk in range(slots):
                hit = (lax.rem(ids_ref[kk, own + m], rows) == target) & (kk < count)
                k = jnp.where(hit, jnp.int32(kk), k)
                weight = jnp.where(hit, jnp.float32(1.0), weight)
            picks.append((m * slots + k, weight))
        for j in range(CS):
            total = p_ref[picks[0][0], j] * picks[0][1]
            for k, weight in picks[1:]:
                total = total + p_ref[k, j] * weight
            send_ref[(j * rows + i) * 128 : (j * rows + i + 1) * 128] = total
        if i == 1:
            pl.semaphore_wait(barrier, partners)
        if i >= 1:
            for j in range(CS):
                route(i - 1, targets[i - 1], j, 0).start()
    for j in range(CS):
        route(rows - 1, targets[-1], j, 0).start()
    for piece in range(1, len(pieces)):
        for i, target in enumerate(targets):
            for j in range(CS):
                route(i, target, j, piece).start()

    wide = place_ref.shape[1]
    sources = CS * rows
    cell_iota = lax.broadcasted_iota(jnp.int32, (nq * cq, wide), 0)
    lane_iota = lax.broadcasted_iota(jnp.int32, (nq * cq, wide), 1)

    def add_source(r, cells):
        for j in range(CS):
            first = (r * cols + lax.rem(col_at + cols - j, cols)) * members
            cell = jnp.int32(-1)
            column = lax.div(ids_ref[j, first], cols)
            for m in range(members):
                for kk in range(slots):
                    if m > 0 and kk < CS:
                        continue
                    ident = ids_ref[kk, first + m]
                    cell = jnp.where(
                        lax.rem(ident, rows) == row_at,
                        lax.div(ident, rows) * cq + column,
                        cell,
                    )
            lane = lane_iota - (j * rows + r)
            cells = jnp.where((lane == 0) | (lane == sources), cell, cells)
        return cells

    cells = lax.fori_loop(0, rows, add_source, jnp.full((nq * cq, wide), -1, jnp.int32))
    place_ref[...] = (cells == cell_iota).astype(jnp.float32).astype(jnp.bfloat16)

    given.wait()
    place = place_ref[...]
    for piece, (start, height) in enumerate(pieces):
        arrived = recv_ref.at[pl.ds(0, sources * height)]
        pltpu.make_async_copy(arrived, arrived, recv_sem.at[piece]).wait()

        def place_rows(step, carry):
            halves = []
            first = start + step * 4
            for a in range(4):
                line = recv_ref[pl.ds(first + a, sources, stride=128), :]
                high = line.astype(jnp.bfloat16)
                low = (line - high.astype(jnp.float32)).astype(jnp.bfloat16)
                halves.append(jnp.concatenate([high, low], axis=0))
            for a in range(0, 4, 2):
                both = jnp.concatenate(halves[a : a + 2], axis=1)
                total = jnp.dot(place, both, preferred_element_type=jnp.float32)
                for d in range(2):
                    out_ref[:, first + a + d] = given_ref[:, first + a + d].astype(
                        jnp.float32
                    ) - total[:, d * 128 : (d + 1) * 128].reshape(nq, cq, 128)
            return carry

        lax.fori_loop(0, height // 4, place_rows, 0)
    sent = send_ref.at[pl.ds(0, (sources - 1) * 128)]
    pltpu.make_async_copy(sent, sent, send_sem).wait()


def write_kernel(result_ref, out_ref, sem):
    copies = []
    count = 8
    height = result_ref.shape[0] // count
    for i in range(count):
        part = pl.ds(i * height, height)
        copies.append(pltpu.make_async_copy(result_ref.at[part], out_ref.at[part], sem))
        copies[-1].start()
    pltpu.make_async_copy(result_ref, out_ref, sem).wait()


def kept(value):
    return pltpu.with_memory_space_constraint(value, pltpu.HBM)


def on_device(rows, cols, block_ids, iface_counts, inv_factor, coupling, boundary_block):
    slots = block_ids.shape[1]
    width = inv_factor.shape[1]
    members = inv_factor.shape[0] // width
    nq, tall, cq, _ = boundary_block.shape
    sources = CS * rows
    pieces = ((0, 96), (96, 32))
    result = pl.pallas_call(
        functools.partial(exchange_kernel, rows, cols, members, slots, width, nq, cq, pieces),
        out_shape=jax.ShapeDtypeStruct(boundary_block.shape, jnp.float32),
        in_specs=[
            pl.BlockSpec(memory_space=pltpu.SMEM),
            pl.BlockSpec(memory_space=pltpu.SMEM),
            pl.BlockSpec(memory_space=pltpu.HBM),
            pl.BlockSpec(memory_space=pltpu.HBM),
            pl.BlockSpec(memory_space=pltpu.HBM),
        ],
        out_specs=pl.BlockSpec(memory_space=pltpu.VMEM),
        scratch_shapes=[
            pltpu.VMEM((members, width, width), jnp.bfloat16),
            pltpu.VMEM((members, width, slots * 128), jnp.bfloat16),
            pltpu.VMEM((members, width, slots * 128), jnp.bfloat16),
            pltpu.VMEM((members * slots, CS, 128, 128), jnp.float32),
            pltpu.VMEM((sources * 128, 128), jnp.float32),
            pltpu.VMEM((sources * 128, 128), jnp.float32),
            pltpu.VMEM(boundary_block.shape, jnp.bfloat16),
            pltpu.VMEM((nq * cq, 2 * sources), jnp.bfloat16),
            pltpu.SemaphoreType.DMA((2 * members,)),
            pltpu.SemaphoreType.DMA,
            pltpu.SemaphoreType.DMA((len(pieces),)),
            pltpu.SemaphoreType.DMA,
        ],
        compiler_params=pltpu.CompilerParams(
            collective_id=0, has_side_effects=True, vmem_limit_bytes=32 * 1024 * 1024
        ),
        name="exchange",
    )(
        kept(block_ids.T),
        kept(iface_counts),
        kept(inv_factor.reshape(members, width, width)),
        kept(coupling.reshape(members, width, slots * 128)),
        kept(boundary_block),
    )
    return pl.pallas_call(
        write_kernel,
        out_shape=jax.ShapeDtypeStruct(boundary_block.shape, jnp.float32),
        in_specs=[pl.BlockSpec(memory_space=pltpu.VMEM)],
        out_specs=pl.BlockSpec(memory_space=pltpu.HBM),
        scratch_shapes=[pltpu.SemaphoreType.DMA],
        compiler_params=pltpu.CompilerParams(vmem_limit_bytes=16 * 1024 * 1024),
        name="writing",
    )(result)


def solution(mesh):
    return jax.shard_map(
        functools.partial(on_device, mesh.shape["row"], mesh.shape["col"]),
        mesh=mesh,
        in_specs=(
            P(),
            P(),
            P(("row", "col"), None),
            P(("row", "col"), None),
            P(None, "row", None, "col"),
        ),
        out_specs=P(None, "row", None, "col"),
        check_vma=False,
    )
```

profile of v0, /device:TPU:1, one launch (start us, length us, event | category | flops | bytes accessed | tf_op | source)
XLA Modules:
  0.0 61.3 jit_solution(11488401679710799264)
XLA Ops:
  0.0 56.7 %exchange.1.result_ref = f32[24,128,8,128]{3,2,1,0:T(8,128)S(1)} custom-call(s32[8,64]{1,0:T(8,128)} %bitcast.5, s32[64]{0:T(128)} %counts_ref.1, bf16[2,472,472]{2,1,0:T(8,128)(2,1)} %bitcast.4, bf16[2,472,1024]{2,1,0:T(8,128)(2,1)} %bitcast.3, bf16[24,128,8,128]{3,2,1,0:T(8,128)(2,1)} %boundary_ref.1), custom_call_target="tpu_custom_call" | custom-call | tf_op jit(solution)/shard_map/exchange/pallas_call | solution.py:202
  56.7 4.6 %writing.1 = f32[24,128,8,128]{3,2,1,0:T(8,128)} custom-call(f32[24,128,8,128]{3,2,1,0:T(8,128)S(1)} %exchange.1.result_ref), custom_call_target="tpu_custom_call" | custom-call | tf_op jit(solution)/shard_map/writing/pallas_call | solution.py:238
where the time goes:
time: 61.5 us; the launch traced here: 61.3 us
  Pallas kernels  61.3 us (100%)
    pallas_call x1, Pallas kernels, on_device(): pl.pallas_call(functools.partial(exchange_kernel, rows, cols, members, sl...  56.7 us
    pallas_call x1, Pallas kernels, on_device(): pl.pallas_call(write_kernel, out_shape=jax.ShapeDtypeStruct(boundary_bloc...  4.6 us

commit v1 on v0

--- a/solution.py
+++ b/solution.py
@@ -15,9 +15,9 @@
     rows, cols, members, slots, width, nq, cq,
     pieces,
     ids_ref, counts_ref, factor_ref, couple_ref, boundary_ref,
-    out_ref,
-    w_ref, k_ref, y_ref, p_ref, send_ref, recv_ref, given_ref, place_ref,
-    load_sem, send_sem, recv_sem, given_sem,
+    head_ref, rest_ref, recv_ref, cells_ref,
+    w_ref, k_ref, y_ref, p_ref, send_ref, given_ref, place_ref, cell_ref,
+    load_sem, send_sem, recv_sem, given_sem, cell_sem,
 ):
     row_at = lax.axis_index("row")
     col_at = lax.axis_index("col")
@@ -74,10 +74,19 @@
                         d * 128 : (d + 1) * 128, j * 128 : (j + 1) * 128
                     ]
 
-    targets = []
-    for i in range(half):
-        targets.append((1 - side) * half + lax.rem(row_at + i, half))
-        targets.append(side * half + lax.rem(row_at + i + 1, half))
+    fourth = rows // 4
+    plane = row_at // fourth
+
+    def within(at, i):
+        return at * fourth + lax.rem(row_at + i, fourth)
+
+    ends = [within(3 * (1 - side), i) for i in range(fourth)]
+    middles = [within(2 - side, i) for i in range(fourth)]
+    mates = [within(side * 2 + 1 - lax.rem(plane, 2), i) for i in range(fourth)]
+    near = [within(plane, i) for i in range(1, fourth)]
+    targets = [t for pair in zip(ends, mates) for t in pair]
+    whole = len(targets)
+    targets += [t for pair in zip(middles, near) for t in pair] + [middles[-1], row_at]
 
     partners = (rows - 1) + (CS - 1) * rows * (2 if cols > 2 else 1)
     def route(i, target, j, piece):
@@ -114,13 +123,14 @@
             pl.semaphore_wait(barrier, partners)
         if i >= 1:
             for j in range(CS):
-                route(i - 1, targets[i - 1], j, 0).start()
+                for piece in range(len(pieces) if i - 1 < whole else 1):
+                    route(i - 1, targets[i - 1], j, piece).start()
     for j in range(CS):
         route(rows - 1, targets[-1], j, 0).start()
     for piece in range(1, len(pieces)):
-        for i, target in enumerate(targets):
+        for i in range(whole, rows):
             for j in range(CS):
-                route(i, target, j, piece).start()
+                route(i, targets[i], j, piece).start()
 
     wide = place_ref.shape[1]
     sources = CS * rows
@@ -142,6 +152,7 @@
                         lax.div(ident, rows) * cq + column,
                         cell,
                     )
+            cell_ref[j * rows + r] = jnp.maximum(cell, 0)
             lane = lane_iota - (j * rows + r)
             cells = jnp.where((lane == 0) | (lane == sources), cell, cells)
         return cells
@@ -149,43 +160,82 @@
     cells = lax.fori_loop(0, rows, add_source, jnp.full((nq * cq, wide), -1, jnp.int32))
     place_ref[...] = (cells == cell_iota).astype(jnp.float32).astype(jnp.bfloat16)
 
+    listed = pltpu.make_async_copy(cell_ref, cells_ref, cell_sem)
+    listed.start()
+
     given.wait()
+    start, height = pieces[1]
+
+    def widen(q, carry):
+        rest_ref[q] = given_ref[q, start:].astype(jnp.float32).reshape(height * cq, 128)
+        return carry
+
+    lax.fori_loop(0, nq, widen, 0)
+    listed.wait()
+
+    def arrive(piece):
+        arrived = recv_ref.at[pl.ds(0, sources * pieces[piece][1])]
+        pltpu.make_async_copy(arrived, arrived, recv_sem.at[piece]).wait()
+
+    arrive(0)
     place = place_ref[...]
-    for piece, (start, height) in enumerate(pieces):
-        arrived = recv_ref.at[pl.ds(0, sources * height)]
-        pltpu.make_async_copy(arrived, arrived, recv_sem.at[piece]).wait()
-
-        def place_rows(step, carry):
-            halves = []
-            first = start + step * 4
-            for a in range(4):
-                line = recv_ref[pl.ds(first + a, sources, stride=128), :]
-                high = line.astype(jnp.bfloat16)
-                low = (line - high.astype(jnp.float32)).astype(jnp.bfloat16)
-                halves.append(jnp.concatenate([high, low], axis=0))
-            for a in range(0, 4, 2):
-                both = jnp.concatenate(halves[a : a + 2], axis=1)
-                total = jnp.dot(place, both, preferred_element_type=jnp.float32)
-                for d in range(2):
-                    out_ref[:, first + a + d] = given_ref[:, first + a + d].astype(
-                        jnp.float32
-                    ) - total[:, d * 128 : (d + 1) * 128].reshape(nq, cq, 128)
-            return carry
-
-        lax.fori_loop(0, height // 4, place_rows, 0)
+
+    def place_rows(step, carry):
+        first = step * 4
+        halves = []
+        for a in range(4):
+            line = recv_ref[pl.ds(first + a, sources, stride=128), :]
+            high = line.astype(jnp.bfloat16)
+            low = (line - high.astype(jnp.float32)).astype(jnp.bfloat16)
+            halves.append(jnp.concatenate([high, low], axis=0))
+        for a in range(0, 4, 2):
+            both = jnp.concatenate(halves[a : a + 2], axis=1)
+            total = jnp.dot(place, both, preferred_element_type=jnp.float32)
+            for d in range(2):
+                head_ref[:, pl.ds((first + a + d) * cq, cq)] = given_ref[:, first + a + d].astype(
+                    jnp.float32
+                ) - total[:, d * 128 : (d + 1) * 128].reshape(nq, cq, 128)
+        return carry
+
+    lax.fori_loop(0, pieces[0][1] // 4, place_rows, 0)
+    arrive(1)
     sent = send_ref.at[pl.ds(0, (sources - 1) * 128)]
     pltpu.make_async_copy(sent, sent, send_sem).wait()
 
 
-def write_kernel(result_ref, out_ref, sem):
-    copies = []
-    count = 8
-    height = result_ref.shape[0] // count
-    for i in range(count):
-        part = pl.ds(i * height, height)
-        copies.append(pltpu.make_async_copy(result_ref.at[part], out_ref.at[part], sem))
-        copies[-1].start()
-    pltpu.make_async_copy(result_ref, out_ref, sem).wait()
+def write_kernel(
+    sources, cq, pieces,
+    head_ref, given_ref, recv_ref, cells_ref,
+    out_ref, rest_ref,
+    cell_ref, cell_sem, sem,
+):
+    listed = pltpu.make_async_copy(cells_ref, cell_ref, cell_sem)
+    listed.start()
+    nq = head_ref.shape[0]
+    split = 2
+    for i in range(split):
+        part = pl.ds(i * (nq // split), nq // split)
+        pltpu.make_async_copy(
+            head_ref.at[part], out_ref.at[part, pl.ds(0, pieces[0][1] * cq)], sem
+        ).start()
+    listed.wait()
+    start, height = pieces[1]
+
+    def settle(s, carry):
+        cell = cell_ref[s]
+        q = lax.div(cell, cq)
+        at = (q, pl.ds(lax.rem(cell, cq), height, stride=cq), slice(None))
+        rest_ref[at] = rest_ref[at] - recv_ref[pl.ds(pl.multiple_of(s * 128, 128) + start, height)]
+        return carry
+
+    lax.fori_loop(0, sources, settle, 0)
+    split = 4
+    for i in range(split):
+        part = pl.ds(i * (nq // split), nq // split)
+        pltpu.make_async_copy(
+            rest_ref.at[part], out_ref.at[part, pl.ds(start * cq, height * cq)], sem
+        ).start()
+    pltpu.make_async_copy(out_ref, out_ref, sem).wait()
 
 
 def kept(value):
@@ -198,10 +248,15 @@
     members = inv_factor.shape[0] // width
     nq, tall, cq, _ = boundary_block.shape
     sources = CS * rows
-    pieces = ((0, 96), (96, 32))
-    result = pl.pallas_call(
+    pieces = ((0, 32), (32, 96))
+    head, rest, landed, cells = pl.pallas_call(
         functools.partial(exchange_kernel, rows, cols, members, slots, width, nq, cq, pieces),
-        out_shape=jax.ShapeDtypeStruct(boundary_block.shape, jnp.float32),
+        out_shape=(
+            jax.ShapeDtypeStruct((nq, pieces[0][1] * cq, 128), jnp.float32),
+            jax.ShapeDtypeStruct((nq, pieces[1][1] * cq, 128), jnp.float32),
+            jax.ShapeDtypeStruct((sources * 128, 128), jnp.float32),
+            jax.ShapeDtypeStruct((sources,), jnp.int32),
+        ),
         in_specs=[
             pl.BlockSpec(memory_space=pltpu.SMEM),
             pl.BlockSpec(memory_space=pltpu.SMEM),
@@ -209,19 +264,25 @@
             pl.BlockSpec(memory_space=pltpu.HBM),
             pl.BlockSpec(memory_space=pltpu.HBM),
         ],
-        out_specs=pl.BlockSpec(memory_space=pltpu.VMEM),
+        out_specs=(
+            pl.BlockSpec(memory_space=pltpu.VMEM),
+            pl.BlockSpec(memory_space=pltpu.VMEM),
+            pl.BlockSpec(memory_space=pltpu.VMEM),
+            pl.BlockSpec(memory_space=pltpu.HBM),
+        ),
         scratch_shapes=[
             pltpu.VMEM((members, width, width), jnp.bfloat16),
             pltpu.VMEM((members, width, slots * 128), jnp.bfloat16),
             pltpu.VMEM((members, width, slots * 128), jnp.bfloat16),
             pltpu.VMEM((members * slots, CS, 128, 128), jnp.float32),
             pltpu.VMEM((sources * 128, 128), jnp.float32),
-            pltpu.VMEM((sources * 128, 128), jnp.float32),
             pltpu.VMEM(boundary_block.shape, jnp.bfloat16),
             pltpu.VMEM((nq * cq, 2 * sources), jnp.bfloat16),
+            pltpu.SMEM((sources,), jnp.int32),
             pltpu.SemaphoreType.DMA((2 * members,)),
             pltpu.SemaphoreType.DMA,
             pltpu.SemaphoreType.DMA((len(pieces),)),
+            pltpu.SemaphoreType.DMA,
             pltpu.SemaphoreType.DMA,
         ],
         compiler_params=pltpu.CompilerParams(
@@ -235,15 +296,32 @@
         kept(coupling.reshape(members, width, slots * 128)),
         kept(boundary_block),
     )
-    return pl.pallas_call(
-        write_kernel,
-        out_shape=jax.ShapeDtypeStruct(boundary_block.shape, jnp.float32),
-        in_specs=[pl.BlockSpec(memory_space=pltpu.VMEM)],
-        out_specs=pl.BlockSpec(memory_space=pltpu.HBM),
-        scratch_shapes=[pltpu.SemaphoreType.DMA],
+    result, _ = pl.pallas_call(
+        functools.partial(write_kernel, sources, cq, pieces),
+        out_shape=(
+            jax.ShapeDtypeStruct((nq, tall * cq, 128), jnp.float32),
+            jax.ShapeDtypeStruct(rest.shape, jnp.float32),
+        ),
+        in_specs=[
+            pl.BlockSpec(memory_space=pltpu.VMEM),
+            pl.BlockSpec(memory_space=pltpu.VMEM),
+            pl.BlockSpec(memory_space=pltpu.VMEM),
+            pl.BlockSpec(memory_space=pltpu.HBM),
+        ],
+        out_specs=(
+            pl.BlockSpec(memory_space=pltpu.HBM),
+            pl.BlockSpec(memory_space=pltpu.VMEM),
+        ),
+        input_output_aliases={1: 1},
+        scratch_shapes=[
+            pltpu.SMEM((sources,), jnp.int32),
+            pltpu.SemaphoreType.DMA,
+            pltpu.SemaphoreType.DMA,
+        ],
         compiler_params=pltpu.CompilerParams(vmem_limit_bytes=16 * 1024 * 1024),
         name="writing",
-    )(result)
+    )(head, rest, landed, cells)
+    return result.reshape(boundary_block.shape)
 
 
 def solution(mesh):

time: 61.5 us -> 58.4 us (0.950)
  the two profiles are of different devices: /device:TPU:1 before, /device:TPU:9 now
where the time goes in v1:
time: 58.4 us; the launch traced here: 57.3 us
  Pallas kernels  57.3 us (98%)
    pallas_call x1, Pallas kernels, on_device(): pl.pallas_call(functools.partial(exchange_kernel, rows, cols, members, sl...  52.4 us
    pallas_call x1, Pallas kernels, on_device(): pl.pallas_call(functools.partial(write_kernel, sources, cq, pieces), out_...  4.97 us

profile of v1, /device:TPU:9, one launch (start us, length us, event | category | flops | bytes accessed | tf_op | source)
XLA Modules:
  0.0 57.3 jit_solution(12066290220819457609)
XLA Ops:
  0.0 52.4 %exchange.1 = (f32[24,256,128]{2,1,0:T(8,128)S(1)}, f32[24,768,128]{2,1,0:T(8,128)S(1)}, f32[4096,128]{1,0:T(8,128)S(1)}, s32[32]{0:T(128)S(1)}) custom-call(s32[8,64]{1,0:T(8,128)} %bitcast.6, s32[64]{0:T(128)} %counts_ref.1, bf16[2,472,472]{2,1,0:T(8,128)(2,1)} %bitcast.5, bf16[2,472,1024]{2,1,0:T(8,128)(2,1)} %bitcast.4, ...), custom_call_target="tpu_custom_call" | custom-call | tf_op jit(solution)/shard_map/exchange/pallas_call | solution.py:252
  52.4 5.0 %writing.1 = (f32[24,1024,128]{2,1,0:T(8,128)}, f32[24,768,128]{2,1,0:T(8,128)S(1)}) custom-call(f32[24,256,128]{2,1,0:T(8,128)S(1)} %get-tuple-element.10.head_ref, f32[24,768,128]{2,1,0:T(8,128)S(1)} %get-tuple-element.11.given_ref, f32[4096,128]{1,0:T(8,128)S(1)} %get-tuple-element.12.recv_ref, ...), custom_call_target="tpu_custom_call", output_to_operand_aliasing={{1}: (1, {})} | custom-call | tf_op jit(solution)/shard_map/writing/pallas_call | solution.py:299

commit v2 on v1

--- a/solution.py
+++ b/solution.py
@@ -17,7 +17,7 @@
     ids_ref, counts_ref, factor_ref, couple_ref, boundary_ref,
     head_ref, rest_ref, recv_ref, cells_ref,
     w_ref, k_ref, y_ref, p_ref, send_ref, given_ref, place_ref, cell_ref,
-    load_sem, send_sem, recv_sem, given_sem, cell_sem,
+    load_sem, send_sem, recv_sem, given_sem, cell_sem, ready_sem,
 ):
     row_at = lax.axis_index("row")
     col_at = lax.axis_index("col")
@@ -26,69 +26,64 @@
 
     loads = []
     for m in range(members):
-        loads.append(
-            (
-                pltpu.make_async_copy(factor_ref.at[m], w_ref.at[m], load_sem.at[2 * m]),
-                pltpu.make_async_copy(couple_ref.at[m], k_ref.at[m], load_sem.at[2 * m + 1]),
+        loads.append([pltpu.make_async_copy(factor_ref.at[m], w_ref.at[m], load_sem.at[m, slots])])
+        for k in range(slots):
+            loads[m].append(
+                pltpu.make_async_copy(
+                    couple_ref.at[m, :, pl.ds(k * 128, 128)],
+                    k_ref.at[m * slots + k],
+                    load_sem.at[m, k],
+                )
             )
-        )
-        for load in loads[-1]:
+        for load in loads[m]:
             load.start()
 
+    fourth = rows // 4
+    plane = row_at // fourth
+    sides = (0, 1) if cols == 2 else (0, 1, cols - 1)
+
+    def within(at, i):
+        return at * fourth + lax.rem(row_at + i, fourth)
+
     barrier = pltpu.get_barrier_semaphore()
-    for r in range(1, rows):
-        other = lax.rem(row_at + r, rows)
-        pl.semaphore_signal(barrier, inc=1, device_id=(other, col_at), device_id_type=MESH)
-    for r in range(rows):
-        for j in range(1, CS):
-            pl.semaphore_signal(
-                barrier, inc=1, device_id=(r, lax.rem(col_at + j, cols)), device_id_type=MESH
-            )
-            if cols > 2:
+    for hop in range(4):
+        for j in sides:
+            if hop or j:
                 pl.semaphore_signal(
-                    barrier, inc=1, device_id=(r, lax.rem(col_at + cols - j, cols)),
+                    barrier, inc=1,
+                    device_id=(
+                        lax.rem(row_at + hop * fourth, rows), lax.rem(col_at + j, cols)
+                    ),
                     device_id_type=MESH,
                 )
-
-    given = pltpu.make_async_copy(boundary_ref, given_ref, given_sem)
-    given.start()
+    for i in range(1, fourth):
+        pl.semaphore_signal(
+            barrier, inc=1, device_id=(within(plane, i), col_at), device_id_type=MESH
+        )
+
+    def columns(m, k):
+        return jnp.concatenate([k_ref[m * slots + k], k_ref[m * slots + k + 1]], axis=1)
 
     own = (row_at * cols + col_at) * members
     for m in range(members):
         for load in loads[m]:
             load.wait()
-        for n in range(0, slots * 128, 256):
-            y_ref[m, :, n : n + 256] = jnp.dot(
-                w_ref[m], k_ref[m, :, n : n + 256], preferred_element_type=jnp.float32
-            ).astype(jnp.bfloat16)
-        for n in range(0, slots, 2):
-            part = lax.dot_general(
-                y_ref[m, :, n * 128 : n * 128 + 256],
-                y_ref[m, :, 0 : CS * 128],
-                (((0,), (0,)), ((), ())),
-                preferred_element_type=jnp.float32,
-            )
-            for d in range(2):
-                for j in range(CS):
-                    p_ref[m * slots + n + d, j] = part[
-                        d * 128 : (d + 1) * 128, j * 128 : (j + 1) * 128
-                    ]
-
-    fourth = rows // 4
-    plane = row_at // fourth
-
-    def within(at, i):
-        return at * fourth + lax.rem(row_at + i, fourth)
+        y_ref[m, :, 0 : CS * 128] = jnp.dot(
+            w_ref[m], columns(m, 0), preferred_element_type=jnp.float32
+        ).astype(jnp.bfloat16)
+    given = pltpu.make_async_copy(boundary_ref, given_ref, given_sem)
+    given.start()
 
     ends = [within(3 * (1 - side), i) for i in range(fourth)]
     middles = [within(2 - side, i) for i in range(fourth)]
     mates = [within(side * 2 + 1 - lax.rem(plane, 2), i) for i in range(fourth)]
     near = [within(plane, i) for i in range(1, fourth)]
-    targets = [t for pair in zip(ends, mates) for t in pair]
+    targets = [ends[0], middles[0]]
+    early = len(targets)
+    targets += [t for pair in zip(mates, ends[1:]) for t in pair] + [mates[-1]]
     whole = len(targets)
-    targets += [t for pair in zip(middles, near) for t in pair] + [middles[-1], row_at]
-
-    partners = (rows - 1) + (CS - 1) * rows * (2 if cols > 2 else 1)
+    targets += [t for pair in zip(near, middles[1:]) for t in pair] + [row_at]
+
     def route(i, target, j, piece):
         start, height = pieces[piece]
         src = send_ref.at[pl.ds((j * rows + i) * 128 + start, height)]
@@ -104,7 +99,12 @@
             device_id_type=MESH,
         )
 
-    for i, target in enumerate(targets):
+    def launch(i):
+        for j in range(CS):
+            for piece in range(len(pieces) if i < whole else 1):
+                route(i, targets[i], j, piece).start()
+
+    def pick(target):
         picks = []
         for m in range(members):
             k, weight = jnp.int32(0), jnp.float32(0.0)
@@ -113,20 +113,67 @@
                 hit = (lax.rem(ids_ref[kk, own + m], rows) == target) & (kk < count)
                 k = jnp.where(hit, jnp.int32(kk), k)
                 weight = jnp.where(hit, jnp.float32(1.0), weight)
-            picks.append((m * slots + k, weight))
+            picks.append((k, weight))
+        return picks
+
+    for i in range(early):
+        total = None
+        for m, (k, weight) in enumerate(pick(targets[i])):
+            block = jnp.dot(
+                w_ref[m],
+                k_ref[m * slots + k],
+                preferred_element_type=jnp.float32,
+            ).astype(jnp.bfloat16)
+            part = lax.dot_general(
+                block,
+                y_ref[m, :, 0 : CS * 128],
+                (((0,), (0,)), ((), ())),
+                preferred_element_type=jnp.float32,
+            ) * weight
+            total = part if total is None else total + part
         for j in range(CS):
-            total = p_ref[picks[0][0], j] * picks[0][1]
-            for k, weight in picks[1:]:
-                total = total + p_ref[k, j] * weight
+            send_ref[(j * rows + i) * 128 : (j * rows + i + 1) * 128] = total[
+                :, j * 128 : (j + 1) * 128
+            ]
+        if i == 0:
+            pl.semaphore_wait(barrier, 4 * len(sides) - 1 + fourth - 1)
+            for n in range(1, fourth):
+                pl.semaphore_signal(
+                    ready_sem, inc=1, device_id=(within(plane, n), col_at), device_id_type=MESH
+                )
+        launch(i)
+
+    for m in range(members):
+        for n in range(CS * 128, slots * 128, 256):
+            y_ref[m, :, n : n + 256] = jnp.dot(
+                w_ref[m], columns(m, n // 128), preferred_element_type=jnp.float32
+            ).astype(jnp.bfloat16)
+        for n in range(0, slots, 2):
+            part = lax.dot_general(
+                y_ref[m, :, n * 128 : n * 128 + 256],
+                y_ref[m, :, 0 : CS * 128],
+                (((0,), (0,)), ((), ())),
+                preferred_element_type=jnp.float32,
+            )
+            for d in range(2):
+                for j in range(CS):
+                    p_ref[m * slots + n + d, j] = part[
+                        d * 128 : (d + 1) * 128, j * 128 : (j + 1) * 128
+                    ]
+
+    for i in range(early, rows):
+        target = targets[i]
+        picks = pick(target)
+        for j in range(CS):
+            total = p_ref[picks[0][0] + 0, j] * picks[0][1]
+            for m in range(1, members):
+                total = total + p_ref[m * slots + picks[m][0], j] * picks[m][1]
             send_ref[(j * rows + i) * 128 : (j * rows + i + 1) * 128] = total
-        if i == 1:
-            pl.semaphore_wait(barrier, partners)
-        if i >= 1:
-            for j in range(CS):
-                for piece in range(len(pieces) if i - 1 < whole else 1):
-                    route(i - 1, targets[i - 1], j, piece).start()
-    for j in range(CS):
-        route(rows - 1, targets[-1], j, 0).start()
+        if i == early:
+            pl.semaphore_wait(ready_sem, fourth - 1)
+        else:
+            launch(i - 1)
+    launch(rows - 1)
     for piece in range(1, len(pieces)):
         for i in range(whole, rows):
             for j in range(CS):
@@ -248,7 +295,7 @@
     members = inv_factor.shape[0] // width
     nq, tall, cq, _ = boundary_block.shape
     sources = CS * rows
-    pieces = ((0, 32), (32, 96))
+    pieces = ((0, 48), (48, 80))
     head, rest, landed, cells = pl.pallas_call(
         functools.partial(exchange_kernel, rows, cols, members, slots, width, nq, cq, pieces),
         out_shape=(
@@ -272,18 +319,19 @@
         ),
         scratch_shapes=[
             pltpu.VMEM((members, width, width), jnp.bfloat16),
-            pltpu.VMEM((members, width, slots * 128), jnp.bfloat16),
+            pltpu.VMEM((members * slots, width, 128), jnp.bfloat16),
             pltpu.VMEM((members, width, slots * 128), jnp.bfloat16),
             pltpu.VMEM((members * slots, CS, 128, 128), jnp.float32),
             pltpu.VMEM((sources * 128, 128), jnp.float32),
             pltpu.VMEM(boundary_block.shape, jnp.bfloat16),
             pltpu.VMEM((nq * cq, 2 * sources), jnp.bfloat16),
             pltpu.SMEM((sources,), jnp.int32),
-            pltpu.SemaphoreType.DMA((2 * members,)),
+            pltpu.SemaphoreType.DMA((members, slots + 1)),
             pltpu.SemaphoreType.DMA,
             pltpu.SemaphoreType.DMA((len(pieces),)),
             pltpu.SemaphoreType.DMA,
             pltpu.SemaphoreType.DMA,
+            pltpu.SemaphoreType.REGULAR,
         ],
         compiler_params=pltpu.CompilerParams(
             collective_id=0, has_side_effects=True, vmem_limit_bytes=32 * 1024 * 1024

time: 58.4 us -> 57.3 us (0.981)
  Pallas kernels: 57.3 us -> 56.6 us
where the time goes in v2:
time: 57.3 us; the launch traced here: 56.6 us
  Pallas kernels  56.6 us (99%)
    pallas_call x1, Pallas kernels, on_device(): pl.pallas_call(functools.partial(exchange_kernel, rows, cols, members, sl...  52 us
    pallas_call x1, Pallas kernels, on_device(): pl.pallas_call(functools.partial(write_kernel, sources, cq, pieces), out_...  4.62 us

profile of v2, /device:TPU:9, one launch (start us, length us, event | category | flops | bytes accessed | tf_op | source)
XLA Modules:
  0.0 56.6 jit_solution(13571305128853269885)
XLA Ops:
  0.0 52.0 %exchange.1 = (f32[24,384,128]{2,1,0:T(8,128)S(1)}, f32[24,640,128]{2,1,0:T(8,128)S(1)}, f32[4096,128]{1,0:T(8,128)S(1)}, s32[32]{0:T(128)S(1)}) custom-call(s32[8,64]{1,0:T(8,128)} %bitcast.6, s32[64]{0:T(128)} %counts_ref.1, bf16[2,472,472]{2,1,0:T(8,128)(2,1)} %bitcast.5, bf16[2,472,1024]{2,1,0:T(8,128)(2,1)} %bitcast.4, ...), custom_call_target="tpu_custom_call" | custom-call | tf_op jit(solution)/shard_map/exchange/pallas_call | solution.py:299
  52.0 4.6 %writing.1 = (f32[24,1024,128]{2,1,0:T(8,128)}, f32[24,640,128]{2,1,0:T(8,128)S(1)}) custom-call(f32[24,384,128]{2,1,0:T(8,128)S(1)} %get-tuple-element.10.head_ref, f32[24,640,128]{2,1,0:T(8,128)S(1)} %get-tuple-element.11.given_ref, f32[4096,128]{1,0:T(8,128)S(1)} %get-tuple-element.12.recv_ref, ...), custom_call_target="tpu_custom_call", output_to_operand_aliasing={{1}: (1, {})} | custom-call | tf_op jit(solution)/shard_map/writing/pallas_call | solution.py:347

commit v3 on v2

--- a/solution.py
+++ b/solution.py
@@ -14,16 +14,22 @@
 def exchange_kernel(
     rows, cols, members, slots, width, nq, cq,
     pieces,
-    ids_ref, counts_ref, factor_ref, couple_ref, boundary_ref,
+    listed_ids_ref, listed_counts_ref, factor_ref, couple_ref, boundary_ref,
     head_ref, rest_ref, recv_ref, cells_ref,
-    w_ref, k_ref, y_ref, p_ref, send_ref, given_ref, place_ref, cell_ref,
-    load_sem, send_sem, recv_sem, given_sem, cell_sem, ready_sem,
+    ids_ref, counts_ref, w_ref, k_ref, y_ref, p_ref, send_ref, given_ref, place_ref, cell_ref,
+    list_sem, load_sem, send_sem, recv_sem, given_sem, cell_sem, ready_sem,
 ):
     row_at = lax.axis_index("row")
     col_at = lax.axis_index("col")
     half = rows // 2
     side = row_at // half
 
+    lists = (
+        pltpu.make_async_copy(listed_ids_ref, ids_ref, list_sem.at[0]),
+        pltpu.make_async_copy(listed_counts_ref, counts_ref, list_sem.at[1]),
+    )
+    for load in lists:
+        load.start()
     loads = []
     for m in range(members):
         loads.append([pltpu.make_async_copy(factor_ref.at[m], w_ref.at[m], load_sem.at[m, slots])])
@@ -31,7 +37,7 @@
             loads[m].append(
                 pltpu.make_async_copy(
                     couple_ref.at[m, :, pl.ds(k * 128, 128)],
-                    k_ref.at[m * slots + k],
+                    k_ref[m].at[k],
                     load_sem.at[m, k],
                 )
             )
@@ -62,18 +68,9 @@
         )
 
     def columns(m, k):
-        return jnp.concatenate([k_ref[m * slots + k], k_ref[m * slots + k + 1]], axis=1)
+        return jnp.concatenate([k_ref[m][k], k_ref[m][k + 1]], axis=1)
 
     own = (row_at * cols + col_at) * members
-    for m in range(members):
-        for load in loads[m]:
-            load.wait()
-        y_ref[m, :, 0 : CS * 128] = jnp.dot(
-            w_ref[m], columns(m, 0), preferred_element_type=jnp.float32
-        ).astype(jnp.bfloat16)
-    given = pltpu.make_async_copy(boundary_ref, given_ref, given_sem)
-    given.start()
-
     ends = [within(3 * (1 - side), i) for i in range(fourth)]
     middles = [within(2 - side, i) for i in range(fourth)]
     mates = [within(side * 2 + 1 - lax.rem(plane, 2), i) for i in range(fourth)]
@@ -116,21 +113,48 @@
             picks.append((k, weight))
         return picks
 
-    for i in range(early):
-        total = None
-        for m, (k, weight) in enumerate(pick(targets[i])):
-            block = jnp.dot(
-                w_ref[m],
-                k_ref[m * slots + k],
-                preferred_element_type=jnp.float32,
-            ).astype(jnp.bfloat16)
-            part = lax.dot_general(
-                block,
-                y_ref[m, :, 0 : CS * 128],
+    for load in lists:
+        load.wait()
+    merged = 1
+    picked = [pick(targets[i]) for i in range(early)]
+    parts = []
+    for m in range(members):
+        for load in loads[m]:
+            load.wait()
+        blocks = [k_ref[m][k] for k in range(CS)]
+        blocks += [k_ref[m][picked[i][m][0]] for i in range(merged)]
+        made = jnp.dot(
+            w_ref[m], jnp.concatenate(blocks, axis=1), preferred_element_type=jnp.float32
+        ).astype(jnp.bfloat16)
+        y_ref[m, :, 0 : CS * 128] = made[:, 0 : CS * 128]
+        parts.append(
+            lax.dot_general(
+                made[:, CS * 128 :],
+                made[:, 0 : CS * 128],
                 (((0,), (0,)), ((), ())),
                 preferred_element_type=jnp.float32,
-            ) * weight
-            total = part if total is None else total + part
+            )
+        )
+    for i in range(early):
+        if i >= merged:
+            made = []
+            for m in range(members):
+                block = jnp.dot(
+                    w_ref[m], k_ref[m][picked[i][m][0]], preferred_element_type=jnp.float32
+                ).astype(jnp.bfloat16)
+                made.append(
+                    lax.dot_general(
+                        block,
+                        y_ref[m, :, 0 : CS * 128],
+                        (((0,), (0,)), ((), ())),
+                        preferred_element_type=jnp.float32,
+                    )
+                )
+        else:
+            made = [part[i * 128 : (i + 1) * 128] for part in parts]
+        total = made[0] * picked[i][0][1]
+        for m in range(1, members):
+            total = total + made[m] * picked[i][m][1]
         for j in range(CS):
             send_ref[(j * rows + i) * 128 : (j * rows + i + 1) * 128] = total[
                 :, j * 128 : (j + 1) * 128
@@ -142,6 +166,9 @@
                     ready_sem, inc=1, device_id=(within(plane, n), col_at), device_id_type=MESH
                 )
         launch(i)
+        if i == 0:
+            given = pltpu.make_async_copy(boundary_ref, given_ref, given_sem)
+            given.start()
 
     for m in range(members):
         for n in range(CS * 128, slots * 128, 256):
@@ -259,12 +286,8 @@
     listed = pltpu.make_async_copy(cells_ref, cell_ref, cell_sem)
     listed.start()
     nq = head_ref.shape[0]
-    split = 2
-    for i in range(split):
-        part = pl.ds(i * (nq // split), nq // split)
-        pltpu.make_async_copy(
-            head_ref.at[part], out_ref.at[part, pl.ds(0, pieces[0][1] * cq)], sem
-        ).start()
+    for q in range(nq):
+        pltpu.make_async_copy(head_ref.at[q], out_ref.at[q, pl.ds(0, pieces[0][1] * cq)], sem).start()
     listed.wait()
     start, height = pieces[1]
 
@@ -276,11 +299,9 @@
         return carry
 
     lax.fori_loop(0, sources, settle, 0)
-    split = 4
-    for i in range(split):
-        part = pl.ds(i * (nq // split), nq // split)
+    for q in range(nq):
         pltpu.make_async_copy(
-            rest_ref.at[part], out_ref.at[part, pl.ds(start * cq, height * cq)], sem
+            rest_ref.at[q], out_ref.at[q, pl.ds(start * cq, height * cq)], sem
         ).start()
     pltpu.make_async_copy(out_ref, out_ref, sem).wait()
 
@@ -305,8 +326,8 @@
             jax.ShapeDtypeStruct((sources,), jnp.int32),
         ),
         in_specs=[
-            pl.BlockSpec(memory_space=pltpu.SMEM),
-            pl.BlockSpec(memory_space=pltpu.SMEM),
+            pl.BlockSpec(memory_space=pltpu.HBM),
+            pl.BlockSpec(memory_space=pltpu.HBM),
             pl.BlockSpec(memory_space=pltpu.HBM),
             pl.BlockSpec(memory_space=pltpu.HBM),
             pl.BlockSpec(memory_space=pltpu.HBM),
@@ -318,14 +339,17 @@
             pl.BlockSpec(memory_space=pltpu.HBM),
         ),
         scratch_shapes=[
+            pltpu.SMEM((slots, block_ids.shape[0]), jnp.int32),
+            pltpu.SMEM((block_ids.shape[0],), jnp.int32),
             pltpu.VMEM((members, width, width), jnp.bfloat16),
-            pltpu.VMEM((members * slots, width, 128), jnp.bfloat16),
+            [pltpu.VMEM((slots, width, 128), jnp.bfloat16)] * members,
             pltpu.VMEM((members, width, slots * 128), jnp.bfloat16),
             pltpu.VMEM((members * slots, CS, 128, 128), jnp.float32),
             pltpu.VMEM((sources * 128, 128), jnp.float32),
             pltpu.VMEM(boundary_block.shape, jnp.bfloat16),
             pltpu.VMEM((nq * cq, 2 * sources), jnp.bfloat16),
             pltpu.SMEM((sources,), jnp.int32),
+            pltpu.SemaphoreType.DMA((2,)),
             pltpu.SemaphoreType.DMA((members, slots + 1)),
             pltpu.SemaphoreType.DMA,
             pltpu.SemaphoreType.DMA((len(pieces),)),

time: 57.3 us -> 56.2 us (0.981)
  Pallas kernels: 56.6 us -> 55.5 us
    pallas_call x1, Pallas kernels: 52 us -> 51 us  [on_device(): pl.pallas_call(functools.partial(exchange_kernel, rows, cols, members, sl...]
where the time goes in v3:
time: 56.2 us; the launch traced here: 55.5 us
  Pallas kernels  55.5 us (99%)
    pallas_call x1, Pallas kernels, on_device(): pl.pallas_call(functools.partial(exchange_kernel, rows, cols, members, sl...  51 us
    pallas_call x1, Pallas kernels, on_device(): pl.pallas_call(functools.partial(write_kernel, sources, cq, pieces), out_...  4.54 us

profile of v3, /device:TPU:9, one launch (start us, length us, event | category | flops | bytes accessed | tf_op | source)
XLA Modules:
  0.0 55.5 jit_solution(16452401228033155744)
XLA Ops:
  0.0 51.0 %exchange.1 = (f32[24,384,128]{2,1,0:T(8,128)S(1)}, f32[24,640,128]{2,1,0:T(8,128)S(1)}, f32[4096,128]{1,0:T(8,128)S(1)}, s32[32]{0:T(128)S(1)}) custom-call(s32[8,64]{1,0:T(8,128)} %bitcast.6, s32[64]{0:T(128)} %listed_counts_ref.1, bf16[2,472,472]{2,1,0:T(8,128)(2,1)} %bitcast.5, bf16[2,472,1024]{2,1,0:T(8,128)(2,1)} %bitcast.4, ...), custom_call_target="tpu_custom_call" | custom-call | tf_op jit(solution)/shard_map/exchange/pallas_call | solution.py:320
  51.0 4.5 %writing.1 = (f32[24,1024,128]{2,1,0:T(8,128)}, f32[24,640,128]{2,1,0:T(8,128)S(1)}) custom-call(f32[24,384,128]{2,1,0:T(8,128)S(1)} %get-tuple-element.10.head_ref, f32[24,640,128]{2,1,0:T(8,128)S(1)} %get-tuple-element.11.given_ref, f32[4096,128]{1,0:T(8,128)S(1)} %get-tuple-element.12.recv_ref, ...), custom_call_target="tpu_custom_call", output_to_operand_aliasing={{1}: (1, {})} | custom-call | tf_op jit(solution)/shard_map/writing/pallas_call | solution.py:371

commit v4 on v3

v4 whole, which is shorter than its diff:
```python
import functools

import jax
import jax.numpy as jnp
from jax import lax
from jax.experimental import pallas as pl
from jax.experimental.pallas import tpu as pltpu
from jax.sharding import PartitionSpec as P

CS = 2
MESH = pl.DeviceIdType.MESH


def around(rows, row_at, at, i):
    fourth = rows // 4
    place = lax.rem(row_at, fourth)
    pair = lax.rem(place // 2 + i // 2, fourth // 2)
    return at * fourth + 2 * pair + lax.rem(place + i, 2)


def is_inner(rows, row_at):
    plane = row_at // (rows // 4)
    return (plane == 1) | (plane == 2)


def exchange_kernel(
    rows, cols, members, slots, width, nq, cq, split,
    listed_ids_ref, listed_counts_ref, factor_ref, couple_ref, boundary_ref,
    head_ref, rest_ref, recv_ref, late_ref, cells_ref,
    ids_ref, counts_ref, w_ref, k_ref, y_ref, p_ref, send_ref, given_ref, cell_ref,
    list_sem, load_sem, send_sem, recv_sem, given_sem, cell_sem, ready_sem,
):
    row_at = lax.axis_index("row")
    col_at = lax.axis_index("col")
    half = rows // 2
    side = row_at // half
    fourth = rows // 4
    plane = row_at // fourth
    inner = is_inner(rows, row_at)
    sides = (0, 1) if cols == 2 else (0, 1, cols - 1)
    sources = CS * rows
    within = functools.partial(around, rows, row_at)

    lists = (
        pltpu.make_async_copy(listed_ids_ref, ids_ref, list_sem.at[0]),
        pltpu.make_async_copy(listed_counts_ref, counts_ref, list_sem.at[1]),
    )
    for load in lists:
        load.start()
    loads = []
    for m in range(members):
        loads.append([pltpu.make_async_copy(factor_ref.at[m], w_ref.at[m], load_sem.at[m, slots])])
        for k in range(slots):
            loads[m].append(
                pltpu.make_async_copy(
                    couple_ref.at[m, :, pl.ds(k * 128, 128)],
                    k_ref[m].at[k],
                    load_sem.at[m, k],
                )
            )
        for load in loads[m]:
            load.start()

    barrier = pltpu.get_barrier_semaphore()
    for hop in range(4):
        for j in sides:
            if hop or j:
                pl.semaphore_signal(
                    barrier, inc=1,
                    device_id=(
                        lax.rem(row_at + hop * fourth, rows), lax.rem(col_at + j, cols)
                    ),
                    device_id_type=MESH,
                )
    for i in range(1, fourth):
        pl.semaphore_signal(
            barrier, inc=1, device_id=(within(plane, i), col_at), device_id_type=MESH
        )

    far_mid = 2 - side

    @pl.when(inner)
    def _():
        for i in range(fourth):
            for j in range(CS):
                at = (j * rows + within(far_mid, i)) * 128
                recv_ref[pl.ds(at, 128)] = jnp.zeros((128, 128), jnp.float32)

    def columns(m, k):
        return jnp.concatenate([k_ref[m][k], k_ref[m][k + 1]], axis=1)

    own = (row_at * cols + col_at) * members
    ends = [within(3 * (1 - side), i) for i in range(fourth)]
    middles = [within(far_mid, i) for i in range(fourth)]
    mates = [within(side * 2 + 1 - lax.rem(plane, 2), i) for i in range(fourth)]
    near = [within(plane, i) for i in range(1, fourth)]
    early = 2
    outer_order = [mates[0], middles[0]]
    for i in range(len(near)):
        outer_order += [mates[i + 1], near[i]]
    outer_order += middles[1:] + ends
    inner_order = [ends[0], mates[0]] + ends[1:]
    for i in range(len(near)):
        inner_order += [mates[i + 1], near[i]]
    inner_order += middles
    targets = [jnp.where(inner, a, b) for a, b in zip(inner_order, outer_order)] + [row_at]
    late = rows - 1 - fourth

    def staged(i, j):
        if late <= i < rows - 1:
            return late_ref, ((i - late) * CS + j) * 128
        return send_ref, (j * rows + i) * 128

    def route(i, target, j):
        ref, at = staged(i, j)
        src = ref.at[pl.ds(at, 128)]
        dst = recv_ref.at[pl.ds((j * rows + row_at) * 128, 128)]
        if j == 0 and i == rows - 1:
            return pltpu.make_async_copy(src, dst, recv_sem)
        return pltpu.make_async_remote_copy(
            src_ref=src,
            dst_ref=dst,
            send_sem=send_sem,
            recv_sem=recv_sem,
            device_id=(target, lax.rem(col_at + j, cols)),
            device_id_type=MESH,
        )

    def launch(i):
        for j in range(CS):
            route(i, targets[i], j).start()

    def pick(target):
        picks = []
        for m in range(members):
            k, weight = jnp.int32(0), jnp.float32(0.0)
            count = counts_ref[own + m]
            for kk in range(slots):
                hit = (lax.rem(ids_ref[kk, own + m], rows) == target) & (kk < count)
                k = jnp.where(hit, jnp.int32(kk), k)
                weight = jnp.where(hit, jnp.float32(1.0), weight)
            picks.append((k, weight))
        return picks

    for load in lists:
        load.wait()
    merged = 1
    picked = [pick(targets[i]) for i in range(early)]
    parts = []
    for m in range(members):
        for load in loads[m]:
            load.wait()
        blocks = [k_ref[m][k] for k in range(CS)]
        blocks += [k_ref[m][picked[i][m][0]] for i in range(merged)]
        made = jnp.dot(
            w_ref[m], jnp.concatenate(blocks, axis=1), preferred_element_type=jnp.float32
        ).astype(jnp.bfloat16)
        y_ref[m, :, 0 : CS * 128] = made[:, 0 : CS * 128]
        parts.append(
            lax.dot_general(
                made[:, CS * 128 :],
                made[:, 0 : CS * 128],
                (((0,), (0,)), ((), ())),
                preferred_element_type=jnp.float32,
            )
        )
    for i in range(early):
        if i >= merged:
            made = []
            for m in range(members):
                block = jnp.dot(
                    w_ref[m], k_ref[m][picked[i][m][0]], preferred_element_type=jnp.float32
                ).astype(jnp.bfloat16)
                made.append(
                    lax.dot_general(
                        block,
                        y_ref[m, :, 0 : CS * 128],
                        (((0,), (0,)), ((), ())),
                        preferred_element_type=jnp.float32,
                    )
                )
        else:
            made = [part[i * 128 : (i + 1) * 128] for part in parts]
        total = made[0] * picked[i][0][1]
        for m in range(1, members):
            total = total + made[m] * picked[i][m][1]
        for j in range(CS):
            send_ref[(j * rows + i) * 128 : (j * rows + i + 1) * 128] = total[
                :, j * 128 : (j + 1) * 128
            ]
        if i == 0:
            pl.semaphore_wait(barrier, 4 * len(sides) - 1 + fourth - 1)
            for n in range(1, fourth):
                pl.semaphore_signal(
                    ready_sem, inc=1, device_id=(within(plane, n), col_at), device_id_type=MESH
                )
        launch(i)
        if i == 0:
            given = pltpu.make_async_copy(boundary_ref, given_ref, given_sem)
            given.start()

    for m in range(members):
        for n in range(CS * 128, slots * 128, 256):
            y_ref[m, :, n : n + 256] = jnp.dot(
                w_ref[m], columns(m, n // 128), preferred_element_type=jnp.float32
            ).astype(jnp.bfloat16)
        for n in range(0, slots, 2):
            part = lax.dot_general(
                y_ref[m, :, n * 128 : n * 128 + 256],
                y_ref[m, :, 0 : CS * 128],
                (((0,), (0,)), ((), ())),
                preferred_element_type=jnp.float32,
            )
            for d in range(2):
                for j in range(CS):
                    p_ref[m * slots + n + d, j] = part[
                        d * 128 : (d + 1) * 128, j * 128 : (j + 1) * 128
                    ]

    for i in range(early, rows):
        picks = pick(targets[i])
        for j in range(CS):
            total = p_ref[picks[0][0], j] * picks[0][1]
            for m in range(1, members):
                total = total + p_ref[m * slots + picks[m][0], j] * picks[m][1]
            ref, at = staged(i, j)
            ref[at : at + 128] = total
        if i == early:
            pl.semaphore_wait(ready_sem, fourth - 1)
        elif i <= late:
            launch(i - 1)
    launch(rows - 1)

    @pl.when(jnp.logical_not(inner))
    def _():
        for i in range(late, rows - 1):
            launch(i)

    def add_source(r, carry):
        for j in range(CS):
            first = (r * cols + lax.rem(col_at + cols - j, cols)) * members
            cell = jnp.int32(0)
            column = lax.div(ids_ref[j, first], cols)
            for m in range(members):
                for kk in range(slots):
                    if m > 0 and kk < CS:
                        continue
                    ident = ids_ref[kk, first + m]
                    cell = jnp.where(
                        lax.rem(ident, rows) == row_at,
                        lax.div(ident, rows) * cq + column,
                        cell,
                    )
            cell_ref[j * rows + r] = cell
        return carry

    lax.fori_loop(0, rows, add_source, 0)
    for i in range(fourth):
        for j in range(CS):
            cell_ref[sources + i * CS + j] = cell_ref[j * rows + within(far_mid, i)]
    listed = pltpu.make_async_copy(cell_ref, cells_ref, cell_sem)
    listed.start()

    given.wait()
    tall = given_ref.shape[1]

    def widen(q, carry):
        head_ref[q] = given_ref[q, :split].astype(jnp.float32).reshape(split * cq, 128)
        rest_ref[q] = given_ref[q, split:].astype(jnp.float32).reshape((tall - split) * cq, 128)
        return carry

    lax.fori_loop(0, nq, widen, 0)
    listed.wait()

    def settled(tiles):
        arrived = recv_ref.at[pl.ds(0, tiles * 128)]
        pltpu.make_async_copy(arrived, arrived, recv_sem).wait()
        sent = send_ref.at[pl.ds(0, (tiles - 1) * 128)]
        pltpu.make_async_copy(sent, sent, send_sem).wait()

    @pl.when(inner)
    def _():
        settled(sources - fourth * CS)

    @pl.when(jnp.logical_not(inner))
    def _():
        settled(sources)


def write_kernel(
    sources, cq, split,
    head_in_ref, rest_in_ref, recv_ref, cells_ref,
    out_ref, head_ref, rest_ref,
    cell_ref, cell_sem, sem,
):
    listed = pltpu.make_async_copy(cells_ref, cell_ref, cell_sem)
    listed.start()
    listed.wait()
    nq = head_ref.shape[0]
    tall = out_ref.shape[1] // cq

    for ref, start, height in ((head_ref, 0, split), (rest_ref, split, tall - split)):

        def settle(s, carry):
            cell = cell_ref[s]
            at = (lax.div(cell, cq), pl.ds(lax.rem(cell, cq), height, stride=cq), slice(None))
            ref[at] = ref[at] - recv_ref[pl.ds(pl.multiple_of(s * 128, 128) + start, height)]
            return carry

        lax.fori_loop(0, sources, settle, 0)
        for q in range(nq):
            pltpu.make_async_copy(
                ref.at[q], out_ref.at[q, pl.ds(start * cq, height * cq)], sem
            ).start()
    pltpu.make_async_copy(out_ref, out_ref, sem).wait()


def late_kernel(rows, cols, late_ref, after_ref, recv_ref, send_sem, recv_sem):
    row_at = lax.axis_index("row")
    col_at = lax.axis_index("col")
    sides = (0, 1) if cols == 2 else (0, 1, cols - 1)
    barrier = pltpu.get_barrier_semaphore()
    partners = [around(rows, row_at, 2 - row_at // (rows // 2), i) for i in range((rows // 4))]

    @pl.when(is_inner(rows, row_at))
    def _():
        for partner in partners:
            for j in sides:
                pl.semaphore_signal(
                    barrier, inc=1, device_id=(partner, lax.rem(col_at + j, cols)),
                    device_id_type=MESH,
                )
        pl.semaphore_wait(barrier, (rows // 4) * len(sides))
        for i, partner in enumerate(partners):
            for j in range(CS):
                part = pl.ds((i * CS + j) * 128, 128)
                pltpu.make_async_remote_copy(
                    src_ref=late_ref.at[part],
                    dst_ref=recv_ref.at[part],
                    send_sem=send_sem,
                    recv_sem=recv_sem,
                    device_id=(partner, lax.rem(col_at + j, cols)),
                    device_id_type=MESH,
                ).start()
        pltpu.make_async_copy(recv_ref, recv_ref, recv_sem).wait()
        pltpu.make_async_copy(late_ref, late_ref, send_sem).wait()


def patch_kernel(
    rows, sources, cq, split,
    result_ref, head_in_ref, rest_in_ref, recv_ref, cells_ref,
    out_ref, head_ref, rest_ref,
    cell_ref, cell_sem, sem,
):
    tall = out_ref.shape[1] // cq
    parts = ((head_ref, 0, split), (rest_ref, split, tall - split))

    @pl.when(is_inner(rows, lax.axis_index("row")))
    def _():
        listed = pltpu.make_async_copy(cells_ref, cell_ref, cell_sem)
        listed.start()
        listed.wait()
        cells = [cell_ref[sources + n] for n in range((rows // 4) * CS)]
        for n, cell in enumerate(cells):
            for ref, start, height in parts:
                at = (lax.div(cell, cq), pl.ds(lax.rem(cell, cq), height, stride=cq), slice(None))
                ref[at] = ref[at] - recv_ref[n * 128 + start : n * 128 + start + height]
        copies = []
        for cell in cells:
            q = lax.div(cell, cq)
            for ref, start, height in parts:
                copies.append(
                    pltpu.make_async_copy(
                        ref.at[q], out_ref.at[q, pl.ds(start * cq, height * cq)], sem
                    )
                )
                copies[-1].start()
        for copy in copies:
            copy.wait()


def kept(value):
    return pltpu.with_memory_space_constraint(value, pltpu.HBM)


def on_device(rows, cols, block_ids, iface_counts, inv_factor, coupling, boundary_block):
    slots = block_ids.shape[1]
    width = inv_factor.shape[1]
    members = inv_factor.shape[0] // width
    nq, tall, cq, _ = boundary_block.shape
    sources = CS * rows
    split = 48
    vmem = pl.BlockSpec(memory_space=pltpu.VMEM)
    hbm = pl.BlockSpec(memory_space=pltpu.HBM)
    head_shape = jax.ShapeDtypeStruct((nq, split * cq, 128), jnp.float32)
    rest_shape = jax.ShapeDtypeStruct((nq, (tall - split) * cq, 128), jnp.float32)
    late_shape = jax.ShapeDtypeStruct(((rows // 4) * CS * 128, 128), jnp.float32)
    result_shape = jax.ShapeDtypeStruct((nq, tall * cq, 128), jnp.float32)
    head, rest, landed, late, cells = pl.pallas_call(
        functools.partial(exchange_kernel, rows, cols, members, slots, width, nq, cq, split),
        out_shape=(
            head_shape,
            rest_shape,
            jax.ShapeDtypeStruct((sources * 128, 128), jnp.float32),
            late_shape,
            jax.ShapeDtypeStruct((sources + (rows // 4) * CS,), jnp.int32),
        ),
        in_specs=[hbm] * 5,
        out_specs=(vmem, vmem, vmem, vmem, hbm),
        scratch_shapes=[
            pltpu.SMEM((slots, block_ids.shape[0]), jnp.int32),
            pltpu.SMEM((block_ids.shape[0],), jnp.int32),
            pltpu.VMEM((members, width, width), jnp.bfloat16),
            [pltpu.VMEM((slots, width, 128), jnp.bfloat16)] * members,
            pltpu.VMEM((members, width, slots * 128), jnp.bfloat16),
            pltpu.VMEM((members * slots, CS, 128, 128), jnp.float32),
            pltpu.VMEM((sources * 128, 128), jnp.float32),
            pltpu.VMEM(boundary_block.shape, jnp.bfloat16),
            pltpu.SMEM((sources + (rows // 4) * CS,), jnp.int32),
            pltpu.SemaphoreType.DMA((2,)),
            pltpu.SemaphoreType.DMA((members, slots + 1)),
            pltpu.SemaphoreType.DMA,
            pltpu.SemaphoreType.DMA,
            pltpu.SemaphoreType.DMA,
            pltpu.SemaphoreType.DMA,
            pltpu.SemaphoreType.REGULAR,
        ],
        compiler_params=pltpu.CompilerParams(
            collective_id=0, has_side_effects=True, vmem_limit_bytes=32 * 1024 * 1024
        ),
        name="exchange",
    )(
        kept(block_ids.T),
        kept(iface_counts),
        kept(inv_factor.reshape(members, width, width)),
        kept(coupling.reshape(members, width, slots * 128)),
        kept(boundary_block),
    )
    local = [
        pltpu.SMEM((sources + (rows // 4) * CS,), jnp.int32),
        pltpu.SemaphoreType.DMA,
        pltpu.SemaphoreType.DMA,
    ]
    result, head, rest = pl.pallas_call(
        functools.partial(write_kernel, sources, cq, split),
        out_shape=(result_shape, head_shape, rest_shape),
        in_specs=[vmem, vmem, vmem, hbm],
        out_specs=(hbm, vmem, vmem),
        input_output_aliases={0: 1, 1: 2},
        scratch_shapes=local,
        compiler_params=pltpu.CompilerParams(vmem_limit_bytes=16 * 1024 * 1024),
        name="writing",
    )(head, rest, landed, cells)
    landed = pl.pallas_call(
        functools.partial(late_kernel, rows, cols),
        out_shape=late_shape,
        in_specs=[vmem, vmem],
        out_specs=vmem,
        scratch_shapes=[pltpu.SemaphoreType.DMA, pltpu.SemaphoreType.DMA],
        compiler_params=pltpu.CompilerParams(
            collective_id=1, has_side_effects=True, vmem_limit_bytes=16 * 1024 * 1024
        ),
        name="late",
    )(late, rest)
    result, _, _ = pl.pallas_call(
        functools.partial(patch_kernel, rows, sources, cq, split),
        out_shape=(result_shape, head_shape, rest_shape),
        in_specs=[hbm, vmem, vmem, vmem, hbm],
        out_specs=(hbm, vmem, vmem),
        input_output_aliases={0: 0, 1: 1, 2: 2},
        scratch_shapes=local,
        compiler_params=pltpu.CompilerParams(vmem_limit_bytes=16 * 1024 * 1024),
        name="patching",
    )(result, head, rest, landed, cells)
    return result.reshape(boundary_block.shape)


def solution(mesh):
    return jax.shard_map(
        functools.partial(on_device, mesh.shape["row"], mesh.shape["col"]),
        mesh=mesh,
        in_specs=(
            P(),
            P(),
            P(("row", "col"), None),
            P(("row", "col"), None),
            P(None, "row", None, "col"),
        ),
        out_specs=P(None, "row", None, "col"),
        check_vma=False,
    )
```

time: 56.2 us -> 55.9 us (level); the launches traced: 55.5 us -> 55.8 us
    pallas_call x1 -> x3, Pallas kernels: 4.54 us -> 24.1 us  [the longest x1 15.7 us: on_device(): pl.pallas_call(functools.partial(late_kernel, rows, cols), out_shape=late...]
    pallas_call x1, Pallas kernels: 51 us -> 31.6 us  [on_device(): pl.pallas_call(functools.partial(exchange_kernel, rows, cols, members, sl...]
where the time goes in v4:
time: 55.9 us; the launch traced here: 55.8 us
  Pallas kernels  55.8 us (100%)
    pallas_call x1, Pallas kernels, on_device(): pl.pallas_call(functools.partial(exchange_kernel, rows, cols, members, sl...  31.6 us
    pallas_call x1, Pallas kernels, on_device(): pl.pallas_call(functools.partial(late_kernel, rows, cols), out_shape=late...  15.7 us
    pallas_call x1, Pallas kernels, on_device(): pl.pallas_call(functools.partial(write_kernel, sources, cq, split), out_s...  5.68 us
    pallas_call x1, Pallas kernels, on_device(): pl.pallas_call(functools.partial(patch_kernel, rows, sources, cq, split),...  2.73 us

profile of v4, /device:TPU:9, one launch (start us, length us, event | category | flops | bytes accessed | tf_op | source)
XLA Modules:
  0.0 55.8 jit_solution(9425960141780869269)
XLA Ops:
  0.0 31.6 %exchange.1 = (f32[24,384,128]{2,1,0:T(8,128)S(1)}, f32[24,640,128]{2,1,0:T(8,128)S(1)}, f32[4096,128]{1,0:T(8,128)S(1)}, f32[1024,128]{1,0:T(8,128)S(1)}, s32[40]{0:T(128)S(1)}) custom-call(s32[8,64]{1,0:T(8,128)} %bitcast.6, s32[64]{0:T(128)} %listed_counts_ref.1, bf16[2,472,472]{2,1,0:T(8,128)(2,1)} %bitcast.5, bf16[2,472,1024]{2,1,0:T(8,128)(2,1)} %bitcast.4, ...), custom_call_target="tpu_custom_call" | custom-call | tf_op jit(solution)/shard_map/exchange/pallas_call | solution.py:399
  31.6 5.7 %writing.1 = (f32[24,1024,128]{2,1,0:T(8,128)}, f32[24,384,128]{2,1,0:T(8,128)S(1)}, f32[24,640,128]{2,1,0:T(8,128)S(1)}) custom-call(f32[24,384,128]{2,1,0:T(8,128)S(1)} %get-tuple-element.14.head_in_ref, f32[24,640,128]{2,1,0:T(8,128)S(1)} %get-tuple-element.15.rest_in_ref, ...), custom_call_target="tpu_custom_call", output_to_operand_aliasing={{1}: (0, {}), {2}: (1, {})} | custom-call | tf_op jit(solution)/shard_map/writing/pallas_call | solution.py:444
  37.3 15.7 %late.1.recv_ref = f32[1024,128]{1,0:T(8,128)S(1)} custom-call(f32[1024,128]{1,0:T(8,128)S(1)} %get-tuple-element.21.late_ref, f32[24,640,128]{2,1,0:T(8,128)S(1)} %get-tuple-element.20.after_ref.rest_in_ref), custom_call_target="tpu_custom_call" | custom-call | tf_op jit(solution)/shard_map/late/pallas_call | solution.py:454
  53.0 2.7 %patching.1 = (f32[24,1024,128]{2,1,0:T(8,128)}, f32[24,384,128]{2,1,0:T(8,128)S(1)}, f32[24,640,128]{2,1,0:T(8,128)S(1)}) custom-call(f32[24,1024,128]{2,1,0:T(8,128)} %get-tuple-element.18.result_ref, f32[24,384,128]{2,1,0:T(8,128)S(1)} %get-tuple-element.19.head_in_ref, ...), custom_call_target="tpu_custom_call", output_to_operand_aliasing={{0}: (0, {}), {1}: (1, {}), {2}: (2, {})} | custom-call | tf_op jit(solution)/shard_map/patching/pallas_call | solution.py:465

commit v5 on v4

--- a/solution.py
+++ b/solution.py
@@ -61,23 +61,27 @@
         for load in loads[m]:
             load.start()
 
+    far_end, far_mid, mate = 3 * (1 - side), 2 - side, side * 2 + 1 - lax.rem(plane, 2)
     barrier = pltpu.get_barrier_semaphore()
-    for hop in range(4):
+
+    def greet(at, i, j):
+        pl.semaphore_signal(
+            barrier, inc=1, device_id=(within(at, i), lax.rem(col_at + j, cols)),
+            device_id_type=MESH,
+        )
+
+    for j in sides:
+        greet(mate, 0, j)
+        greet(far_mid, 0, j)
+        if j:
+            greet(plane, 0, j)
+
+    @pl.when(inner)
+    def _():
         for j in sides:
-            if hop or j:
-                pl.semaphore_signal(
-                    barrier, inc=1,
-                    device_id=(
-                        lax.rem(row_at + hop * fourth, rows), lax.rem(col_at + j, cols)
-                    ),
-                    device_id_type=MESH,
-                )
-    for i in range(1, fourth):
-        pl.semaphore_signal(
-            barrier, inc=1, device_id=(within(plane, i), col_at), device_id_type=MESH
-        )
-
-    far_mid = 2 - side
+            greet(far_end, 0, j)
+        for i in range(1, fourth):
+            greet(plane, i, 0)
 
     @pl.when(inner)
     def _():
@@ -90,18 +94,16 @@
         return jnp.concatenate([k_ref[m][k], k_ref[m][k + 1]], axis=1)
 
     own = (row_at * cols + col_at) * members
-    ends = [within(3 * (1 - side), i) for i in range(fourth)]
+    ends = [within(far_end, i) for i in range(fourth)]
     middles = [within(far_mid, i) for i in range(fourth)]
-    mates = [within(side * 2 + 1 - lax.rem(plane, 2), i) for i in range(fourth)]
+    mates = [within(mate, i) for i in range(fourth)]
     near = [within(plane, i) for i in range(1, fourth)]
     early = 2
     outer_order = [mates[0], middles[0]]
-    for i in range(len(near)):
-        outer_order += [mates[i + 1], near[i]]
-    outer_order += middles[1:] + ends
-    inner_order = [ends[0], mates[0]] + ends[1:]
-    for i in range(len(near)):
-        inner_order += [mates[i + 1], near[i]]
+    for i in range(1, fourth - 1):
+        outer_order += [mates[i], near[i - 1]]
+    outer_order += middles[1:] + [mates[-1], near[-1]] + ends
+    inner_order = [ends[0], mates[0]] + ends[1:] + near + mates[1:]
     inner_order += middles
     targets = [jnp.where(inner, a, b) for a, b in zip(inner_order, outer_order)] + [row_at]
     late = rows - 1 - fourth
@@ -189,11 +191,16 @@
                 :, j * 128 : (j + 1) * 128
             ]
         if i == 0:
-            pl.semaphore_wait(barrier, 4 * len(sides) - 1 + fourth - 1)
-            for n in range(1, fourth):
-                pl.semaphore_signal(
-                    ready_sem, inc=1, device_id=(within(plane, n), col_at), device_id_type=MESH
-                )
+            met = 3 * len(sides) - 1
+            pl.semaphore_wait(barrier, jnp.where(inner, met + len(sides) + fourth - 1, met))
+
+            @pl.when(inner)
+            def _():
+                for n in range(1, fourth):
+                    pl.semaphore_signal(
+                        ready_sem, inc=1, device_id=(within(plane, n), col_at), device_id_type=MESH
+                    )
+
         launch(i)
         if i == 0:
             given = pltpu.make_async_copy(boundary_ref, given_ref, given_sem)
@@ -226,7 +233,14 @@
             ref, at = staged(i, j)
             ref[at : at + 128] = total
         if i == early:
-            pl.semaphore_wait(ready_sem, fourth - 1)
+            pl.semaphore_wait(ready_sem, jnp.where(inner, fourth - 1, 1))
+
+            @pl.when(inner)
+            def _():
+                pl.semaphore_signal(
+                    ready_sem, inc=1, device_id=(within(mate, 0), col_at), device_id_type=MESH
+                )
+
         elif i <= late:
             launch(i - 1)
     launch(rows - 1)
@@ -350,17 +364,18 @@
     rows, sources, cq, split,
     result_ref, head_in_ref, rest_in_ref, recv_ref, cells_ref,
     out_ref, head_ref, rest_ref,
-    cell_ref, cell_sem, sem,
+    sem,
 ):
     tall = out_ref.shape[1] // cq
     parts = ((head_ref, 0, split), (rest_ref, split, tall - split))
 
     @pl.when(is_inner(rows, lax.axis_index("row")))
     def _():
-        listed = pltpu.make_async_copy(cells_ref, cell_ref, cell_sem)
-        listed.start()
-        listed.wait()
-        cells = [cell_ref[sources + n] for n in range((rows // 4) * CS)]
+        listed = cells_ref[...]
+        lane = lax.broadcasted_iota(jnp.int32, listed.shape, 0)
+        cells = [
+            jnp.sum(jnp.where(lane == sources + n, listed, 0)) for n in range((rows // 4) * CS)
+        ]
         for n, cell in enumerate(cells):
             for ref, start, height in parts:
                 at = (lax.div(cell, cq), pl.ds(lax.rem(cell, cq), height, stride=cq), slice(None))
@@ -465,10 +480,10 @@
     result, _, _ = pl.pallas_call(
         functools.partial(patch_kernel, rows, sources, cq, split),
         out_shape=(result_shape, head_shape, rest_shape),
-        in_specs=[hbm, vmem, vmem, vmem, hbm],
+        in_specs=[hbm, vmem, vmem, vmem, vmem],
         out_specs=(hbm, vmem, vmem),
         input_output_aliases={0: 0, 1: 1, 2: 2},
-        scratch_shapes=local,
+        scratch_shapes=local[2:],
         compiler_params=pltpu.CompilerParams(vmem_limit_bytes=16 * 1024 * 1024),
         name="patching",
     )(result, head, rest, landed, cells)

time: 55.9 us -> 55.6 us (level)
    pallas_call x1, Pallas kernels: 15.7 us -> 16.6 us  [on_device(): pl.pallas_call(functools.partial(late_kernel, rows, cols), out_shape=late...]
    pallas_call x1, Pallas kernels: 31.6 us -> 30.9 us  [on_device(): pl.pallas_call(functools.partial(exchange_kernel, rows, cols, members, sl...]
where the time goes in v5:
time: 55.6 us; the launch traced here: 55.5 us
  Pallas kernels  55.4 us (100%)
    pallas_call x1, Pallas kernels, on_device(): pl.pallas_call(functools.partial(exchange_kernel, rows, cols, members, sl...  30.9 us
    pallas_call x1, Pallas kernels, on_device(): pl.pallas_call(functools.partial(late_kernel, rows, cols), out_shape=late...  16.6 us
    pallas_call x1, Pallas kernels, on_device(): pl.pallas_call(functools.partial(write_kernel, sources, cq, split), out_s...  5.68 us
    pallas_call x1, Pallas kernels, on_device(): pl.pallas_call(functools.partial(patch_kernel, rows, sources, cq, split),...  2.26 us

profile of v5, /device:TPU:9, one launch (start us, length us, event | category | flops | bytes accessed | tf_op | source)
XLA Modules:
  0.0 55.5 jit_solution(17459804554208287721)
XLA Ops:
  0.0 30.9 %exchange.1 = (f32[24,384,128]{2,1,0:T(8,128)S(1)}, f32[24,640,128]{2,1,0:T(8,128)S(1)}, f32[4096,128]{1,0:T(8,128)S(1)}, f32[1024,128]{1,0:T(8,128)S(1)}, s32[40]{0:T(128)S(1)}) custom-call(s32[8,64]{1,0:T(8,128)} %bitcast.6, s32[64]{0:T(128)} %listed_counts_ref.1, bf16[2,472,472]{2,1,0:T(8,128)(2,1)} %bitcast.5, bf16[2,472,1024]{2,1,0:T(8,128)(2,1)} %bitcast.4, ...), custom_call_target="tpu_custom_call" | custom-call | tf_op jit(solution)/shard_map/exchange/pallas_call | solution.py:414
  30.9 5.7 %writing.1 = (f32[24,1024,128]{2,1,0:T(8,128)}, f32[24,384,128]{2,1,0:T(8,128)S(1)}, f32[24,640,128]{2,1,0:T(8,128)S(1)}) custom-call(f32[24,384,128]{2,1,0:T(8,128)S(1)} %get-tuple-element.14.head_in_ref, f32[24,640,128]{2,1,0:T(8,128)S(1)} %get-tuple-element.15.rest_in_ref, ...), custom_call_target="tpu_custom_call", output_to_operand_aliasing={{1}: (0, {}), {2}: (1, {})} | custom-call | tf_op jit(solution)/shard_map/writing/pallas_call | solution.py:459
  36.6 16.6 %late.1.recv_ref = f32[1024,128]{1,0:T(8,128)S(1)} custom-call(f32[1024,128]{1,0:T(8,128)S(1)} %get-tuple-element.21.late_ref, f32[24,640,128]{2,1,0:T(8,128)S(1)} %get-tuple-element.20.after_ref.rest_in_ref), custom_call_target="tpu_custom_call" | custom-call | tf_op jit(solution)/shard_map/late/pallas_call | solution.py:469
  53.2 2.3 %patching.1 = (f32[24,1024,128]{2,1,0:T(8,128)}, f32[24,384,128]{2,1,0:T(8,128)S(1)}, f32[24,640,128]{2,1,0:T(8,128)S(1)}) custom-call(f32[24,1024,128]{2,1,0:T(8,128)} %get-tuple-element.18.result_ref, f32[24,384,128]{2,1,0:T(8,128)S(1)} %get-tuple-element.19.head_in_ref, ...), custom_call_target="tpu_custom_call", output_to_operand_aliasing={{0}: (0, {}), {1}: (1, {}), {2}: (2, {})} | custom-call | tf_op jit(solution)/shard_map/patching/pallas_call | solution.py:480

commit v6 on v5

--- a/solution.py
+++ b/solution.py
@@ -49,15 +49,8 @@
         load.start()
     loads = []
     for m in range(members):
-        loads.append([pltpu.make_async_copy(factor_ref.at[m], w_ref.at[m], load_sem.at[m, slots])])
-        for k in range(slots):
-            loads[m].append(
-                pltpu.make_async_copy(
-                    couple_ref.at[m, :, pl.ds(k * 128, 128)],
-                    k_ref[m].at[k],
-                    load_sem.at[m, k],
-                )
-            )
+        loads.append([pltpu.make_async_copy(factor_ref.at[m], w_ref.at[m], load_sem.at[m, 1])])
+        loads[m].append(pltpu.make_async_copy(couple_ref.at[m], k_ref.at[m], load_sem.at[m, 0]))
         for load in loads[m]:
             load.start()
 
@@ -90,8 +83,14 @@
                 at = (j * rows + within(far_mid, i)) * 128
                 recv_ref[pl.ds(at, 128)] = jnp.zeros((128, 128), jnp.float32)
 
+    def chosen(m, k):
+        block = k_ref[m, :, 0:128]
+        for kk in range(1, slots):
+            block = jnp.where(k == kk, k_ref[m, :, kk * 128 : kk * 128 + 128], block)
+        return block
+
     def columns(m, k):
-        return jnp.concatenate([k_ref[m][k], k_ref[m][k + 1]], axis=1)
+        return k_ref[m, :, k * 128 : k * 128 + 256]
 
     own = (row_at * cols + col_at) * members
     ends = [within(far_end, i) for i in range(fourth)]
@@ -152,8 +151,7 @@
     for m in range(members):
         for load in loads[m]:
             load.wait()
-        blocks = [k_ref[m][k] for k in range(CS)]
-        blocks += [k_ref[m][picked[i][m][0]] for i in range(merged)]
+        blocks = [k_ref[m, :, 0 : CS * 128]] + [chosen(m, picked[i][m][0]) for i in range(merged)]
         made = jnp.dot(
             w_ref[m], jnp.concatenate(blocks, axis=1), preferred_element_type=jnp.float32
         ).astype(jnp.bfloat16)
@@ -171,7 +169,7 @@
             made = []
             for m in range(members):
                 block = jnp.dot(
-                    w_ref[m], k_ref[m][picked[i][m][0]], preferred_element_type=jnp.float32
+                    w_ref[m], chosen(m, picked[i][m][0]), preferred_element_type=jnp.float32
                 ).astype(jnp.bfloat16)
                 made.append(
                     lax.dot_general(
@@ -206,6 +204,14 @@
             given = pltpu.make_async_copy(boundary_ref, given_ref, given_sem)
             given.start()
 
+    pl.semaphore_wait(ready_sem, jnp.where(inner, fourth - 1, 1))
+
+    @pl.when(inner)
+    def _():
+        pl.semaphore_signal(
+            ready_sem, inc=1, device_id=(within(mate, 0), col_at), device_id_type=MESH
+        )
+
     for m in range(members):
         for n in range(CS * 128, slots * 128, 256):
             y_ref[m, :, n : n + 256] = jnp.dot(
@@ -232,16 +238,7 @@
                 total = total + p_ref[m * slots + picks[m][0], j] * picks[m][1]
             ref, at = staged(i, j)
             ref[at : at + 128] = total
-        if i == early:
-            pl.semaphore_wait(ready_sem, jnp.where(inner, fourth - 1, 1))
-
-            @pl.when(inner)
-            def _():
-                pl.semaphore_signal(
-                    ready_sem, inc=1, device_id=(within(mate, 0), col_at), device_id_type=MESH
-                )
-
-        elif i <= late:
+        if early < i <= late:
             launch(i - 1)
     launch(rows - 1)
 
@@ -426,14 +423,14 @@
             pltpu.SMEM((slots, block_ids.shape[0]), jnp.int32),
             pltpu.SMEM((block_ids.shape[0],), jnp.int32),
             pltpu.VMEM((members, width, width), jnp.bfloat16),
-            [pltpu.VMEM((slots, width, 128), jnp.bfloat16)] * members,
+            pltpu.VMEM((members, width, slots * 128), jnp.bfloat16),
             pltpu.VMEM((members, width, slots * 128), jnp.bfloat16),
             pltpu.VMEM((members * slots, CS, 128, 128), jnp.float32),
             pltpu.VMEM((sources * 128, 128), jnp.float32),
             pltpu.VMEM(boundary_block.shape, jnp.bfloat16),
             pltpu.SMEM((sources + (rows // 4) * CS,), jnp.int32),
             pltpu.SemaphoreType.DMA((2,)),
-            pltpu.SemaphoreType.DMA((members, slots + 1)),
+            pltpu.SemaphoreType.DMA((members, 2)),
             pltpu.SemaphoreType.DMA,
             pltpu.SemaphoreType.DMA,
             pltpu.SemaphoreType.DMA,

time: 55.6 us -> 55.6 us (level)
  no operation moved by 1% of the time
where the time goes in v6:
time: 55.6 us; the launch traced here: 55.5 us
  Pallas kernels  55.5 us (100%)
    pallas_call x1, Pallas kernels, on_device(): pl.pallas_call(functools.partial(exchange_kernel, rows, cols, members, sl...  30.5 us
    pallas_call x1, Pallas kernels, on_device(): pl.pallas_call(functools.partial(late_kernel, rows, cols), out_shape=late...  17 us
    pallas_call x1, Pallas kernels, on_device(): pl.pallas_call(functools.partial(write_kernel, sources, cq, split), out_s...  5.68 us
    pallas_call x1, Pallas kernels, on_device(): pl.pallas_call(functools.partial(patch_kernel, rows, sources, cq, split),...  2.26 us

profile of v6, /device:TPU:9, one launch (start us, length us, event | category | flops | bytes accessed | tf_op | source)
XLA Modules:
  0.0 55.5 jit_solution(8603532516942019936)
XLA Ops:
  0.0 30.5 %exchange.1 = (f32[24,384,128]{2,1,0:T(8,128)S(1)}, f32[24,640,128]{2,1,0:T(8,128)S(1)}, f32[4096,128]{1,0:T(8,128)S(1)}, f32[1024,128]{1,0:T(8,128)S(1)}, s32[40]{0:T(128)S(1)}) custom-call(s32[8,64]{1,0:T(8,128)} %bitcast.6, s32[64]{0:T(128)} %listed_counts_ref.1, bf16[2,472,472]{2,1,0:T(8,128)(2,1)} %bitcast.5, bf16[2,472,1024]{2,1,0:T(8,128)(2,1)} %bitcast.4, ...), custom_call_target="tpu_custom_call" | custom-call | tf_op jit(solution)/shard_map/exchange/pallas_call | solution.py:411
  30.5 5.7 %writing.1 = (f32[24,1024,128]{2,1,0:T(8,128)}, f32[24,384,128]{2,1,0:T(8,128)S(1)}, f32[24,640,128]{2,1,0:T(8,128)S(1)}) custom-call(f32[24,384,128]{2,1,0:T(8,128)S(1)} %get-tuple-element.14.head_in_ref, f32[24,640,128]{2,1,0:T(8,128)S(1)} %get-tuple-element.15.rest_in_ref, ...), custom_call_target="tpu_custom_call", output_to_operand_aliasing={{1}: (0, {}), {2}: (1, {})} | custom-call | tf_op jit(solution)/shard_map/writing/pallas_call | solution.py:456
  36.2 17.0 %late.1.recv_ref = f32[1024,128]{1,0:T(8,128)S(1)} custom-call(f32[1024,128]{1,0:T(8,128)S(1)} %get-tuple-element.21.late_ref, f32[24,640,128]{2,1,0:T(8,128)S(1)} %get-tuple-element.20.after_ref.rest_in_ref), custom_call_target="tpu_custom_call" | custom-call | tf_op jit(solution)/shard_map/late/pallas_call | solution.py:466
  53.2 2.3 %patching.1 = (f32[24,1024,128]{2,1,0:T(8,128)}, f32[24,384,128]{2,1,0:T(8,128)S(1)}, f32[24,640,128]{2,1,0:T(8,128)S(1)}) custom-call(f32[24,1024,128]{2,1,0:T(8,128)} %get-tuple-element.18.result_ref, f32[24,384,128]{2,1,0:T(8,128)S(1)} %get-tuple-element.19.head_in_ref, ...), custom_call_target="tpu_custom_call", output_to_operand_aliasing={{0}: (0, {}), {1}: (1, {}), {2}: (2, {})} | custom-call | tf_op jit(solution)/shard_map/patching/pallas_call | solution.py:477
